TPU v7x, 32 devices: a whole 2x2x4 slice. The times are simulated.
32 devices in a mesh: cuts: 8 (over z, x), mode: 4 (over y, core).
Axes of the slice: x: 2, y: 2, z: 4, core: 2. Of those that a mesh axis runs over, the one named last changes fastest.
Arguments:
- sliced_state: bfloat16 [8, 16, 4, 128, 2, 128], P(None, 'cuts', None, 'mode'), may hold values from -0.75 to 0.75
- gate_blocks: bfloat16 [32, 2, 128, 128], P('cuts'), may hold values from -0.375 to 0.375
- gate_slot: int32 [32], replicated, may hold values from 0 to 31, each once
- samples: int32 [8, 4096], replicated, may hold values from 0 to 65535
Outputs:
- amplitudes: float32 [32, 128, 2, 128], P('cuts', 'mode')
- sample_probs: float32 [8, 4096], replicated
- xeb_score: float32 [8], replicated
Inputs may be any that keep to these rules, and one draw needn't show every extreme that they name: `gate_slot`: a permutation: every gate block has its own row of gate_blocks. `samples`: flat index s * 128 * 128 + p * 128 + q.
All inputs are finite; a program needn't handle non-finite values.
Results may differ from a plain program's by a relative error of at most 0.022.
Values may be sent and summed in bfloat16 or wider, within the bound.
A program may use at most 64 MiB of HBM per device.

v0:
```python
import jax
import jax.numpy as jnp
from jax import lax
from jax.sharding import PartitionSpec as P


def from_root(array, axis, root):
    mine = lax.axis_index(axis) == root
    return lax.psum(jnp.where(mine, array, jnp.zeros_like(array)), axis)


def apply_gates(tensor, blocks):
    real_part = blocks[:, 0]
    imag_part = blocks[:, 1]
    stacked = jnp.concatenate(
        [
            jnp.concatenate([real_part, imag_part], axis=2),
            jnp.concatenate([-imag_part, real_part], axis=2),
        ],
        axis=1,
    )
    layout = tensor.shape
    flattened = tensor.reshape(layout[0], -1, 2 * layout[-1])
    product = jnp.einsum("crk,ckn->crn", flattened, stacked, preferred_element_type=jnp.float32)
    return product.astype(jnp.bfloat16).reshape(layout)


def select_rows(table, wanted):
    count = table.shape[0]
    onehot = (wanted[:, None] == jnp.arange(count, dtype=jnp.int32)[None, :]).astype(table.dtype)
    picked = jnp.dot(onehot, table.reshape(count, -1), preferred_element_type=jnp.float32)
    return picked.astype(table.dtype).reshape((wanted.shape[0],) + table.shape[1:])


def on_device(sliced_state, gate_blocks, gate_slot, samples):
    circuits = sliced_state.shape[0]
    spectator = sliced_state.shape[2]
    width = sliced_state.shape[5]
    held_count = gate_blocks.shape[0]
    layer_count = gate_slot.shape[0] // (2 * circuits)
    circuit_ids = jnp.arange(circuits, dtype=jnp.int32)
    tensor = lax.all_to_all(sliced_state, "mode", split_axis=0, concat_axis=3, tiled=True)
    local_count = tensor.shape[0]
    local_ids = lax.axis_index("mode") * local_count + jnp.arange(local_count, dtype=jnp.int32)

    def fetch_one(position):
        held_block = select_rows(gate_blocks, jnp.reshape(position % held_count, (1,)))[0]
        return from_root(held_block, "cuts", position // held_count)

    def fetch_gates(layer_index, gate_kind):
        fetched = []
        for circuit in range(local_count):
            fetched.append(
                fetch_one(
                    gate_slot[(local_ids[circuit] * layer_count + layer_index) * 2 + gate_kind]
                )
            )
        return jnp.stack(fetched, axis=0)

    for layer_index in range(layer_count):
        tensor = apply_gates(tensor, fetch_gates(layer_index, 0))
        tensor = jnp.swapaxes(tensor, 3, 5)
        tensor = apply_gates(tensor, fetch_gates(layer_index, 1))
        tensor = jnp.swapaxes(tensor, 3, 5)
    summed = jnp.sum(tensor.astype(jnp.float32), axis=1)
    summed = lax.all_to_all(
        summed.astype(jnp.bfloat16), "mode", split_axis=2, concat_axis=0, tiled=True
    ).astype(summed.dtype)
    local_rows = summed.shape[2]
    summed = summed.reshape(circuits * spectator, local_rows, 2, width)
    amplitudes = lax.psum_scatter(
        summed.astype(jnp.bfloat16), "cuts", scatter_dimension=0, tiled=True
    ).astype(jnp.float32)
    row_count = amplitudes.shape[0]
    first_row = lax.axis_index("cuts") * row_count
    first_col = lax.axis_index("mode") * local_rows
    magnitude = amplitudes[:, :, 0, :] ** 2 + amplitudes[:, :, 1, :] ** 2
    row_sums = jnp.sum(magnitude, axis=(1, 2))
    owner_circuit = (first_row + jnp.arange(row_count, dtype=jnp.int32)) // spectator
    norm_part = jnp.sum(
        jnp.where(owner_circuit[None, :] == circuit_ids[:, None], row_sums[None, :], 0.0), axis=1
    )
    plane_size = width * width
    spec_index = samples // plane_size
    row_index = samples // width % width
    col_index = samples % width
    local_row = circuit_ids[:, None] * spectator + spec_index - first_row
    local_col = row_index - first_col
    is_owned = (
        (local_row >= 0) & (local_row < row_count) & (local_col >= 0) & (local_col < local_rows)
    )
    cell_index = jnp.where(is_owned, local_row * local_rows + local_col, -1)
    cell_count = row_count * local_rows
    cell_onehot = (
        cell_index[:, :, None] == jnp.arange(cell_count, dtype=jnp.int32)[None, None, :]
    ).astype(jnp.float32)
    picked_rows = jnp.einsum(
        "csr,rw->csw",
        cell_onehot,
        magnitude.reshape(cell_count, width),
        precision=lax.Precision.HIGHEST,
    )
    col_match = col_index[:, :, None] == jnp.arange(width, dtype=jnp.int32)[None, None, :]
    sample_mass = jnp.sum(jnp.where(col_match, picked_rows, 0.0), axis=2)
    dimension_scale = float(spectator * plane_size)
    norm_total = lax.psum(norm_part, ("cuts", "mode"))
    sample_probs = lax.psum(sample_mass * dimension_scale / norm_total[:, None], ("cuts", "mode"))
    xeb_score = jnp.mean(sample_probs, axis=1)
    return (amplitudes, sample_probs, xeb_score)


def solution(mesh):
    in_specs = (P(None, "cuts", None, "mode", None, None), P("cuts", None, None, None), P(), P())
    out_specs = (P("cuts", "mode", None, None), P(), P())
    return jax.shard_map(
        on_device, mesh=mesh, in_specs=in_specs, out_specs=out_specs, check_vma=False
    )
```

profile of v0, /device:TPU:0, one launch (start us, length us, event | category | flops | bytes accessed | tf_op | source)
XLA Modules:
  0.0 402.5 jit_solution(14701239896464762398)
XLA Ops:
  10.4 1.6 fusion.73
  32.4 1.2 copy.56
  41.5 4.3 %all-to-all-start = ((bf16[8,2,4,32,2,128]{5,4,3,2,1,0:T(2,128)(2,1)}), bf16[8,2,4,32,2,128]{5,4,3,2,1,0:T(2,128)(2,1)S(1)}, u32[]{:S(2)}, u32[]{:S(2)}) async-start(bf16[8,2,4,32,2,128]{5,4,3,2,1,0:T(2,128)(2,1)} %param.4), calls=%async_computation | async-start | bytes 2097152 | tf_op jit(solution)/shard_map/all_to_all | solution.py:42
  45.8 72.8 %all-reduce.6.cloned.1.call-done = (bf16[1,2,128,128]{2,3,0,1:T(8,128)(2,1)}, bf16[1,2,128,128]{2,3,0,1:T(8,128)(2,1)}, bf16[1,2,128,128]{3,2,0,1:T(8,128)(2,1)}...) async-done(((bf16[1,2,128,128]{2,3,0,1:T(8,128)(2,1)}, ...) | async-done | bytes 524304 | tf_op jit(solution)/shard_map/psum | solution.py:9
  118.6 0.9 constant_dynamic-update-slice_fusion.1
  119.5 0.9 constant_dynamic-update-slice_fusion
  120.4 0.8 constant_dynamic-update-slice_fusion.3
  121.2 0.8 constant_dynamic-update-slice_fusion.5
  122.1 0.9 constant_dynamic-update-slice_fusion.2
  123.1 1.2 copy.55
  125.5 0.8 reshape.306
  126.3 1.1 copy.42
  128.9 1.2 copy.43
  131.5 1.2 copy.44
  134.2 2.4 reduce_sum.50
  137.4 11.4 %all_to_all.33 = bf16[2,4,128,2,128]{4,3,1,0,2:T(2,128)(2,1)S(1)} all-to-all(bf16[2,4,128,2,128]{4,3,1,0,2:T(2,128)(2,1)S(1)} %copy.45), channel_id=1, replica_groups=mesh['cuts'=8,'mode'=4] {'mode'}, dimensions={2} | all-to-all | bytes 1048576 | tf_op jit(solution)/shard_map/all_to_all | solution.py:66
  148.9 0.8 copy.47
  149.9 61.7 %reduce-scatter.2.cloned.1.call-done = bf16[4,32,2,128]{3,1,2,0:T(8,128)(2,1)} async-done(((bf16[32,32,2,128]{3,1,2,0:T(8,128)(2,1)}), bf16[4,32,2,128]{3,1,2,0:T(8,128)(2,1)}) %reduce-scatter.2.cloned.1.call-update) | async-done | bytes 65552 | tf_op jit(solution)/shard_map/reduce_scatter | solution.py:71
  211.5 0.8 convert_element_type.77
  212.9 40.1 %psum.78 = f32[8]{0:T(128)S(1)} all-reduce(f32[8]{0:T(128)S(1)} %select_reduce_fusion.1), channel_id=1, replica_groups=mesh['cuts'=8,'mode'=4] {'cuts','mode'}, use_global_device_ids=true, to_apply=%region_13.14 | all-reduce | flops 8 | bytes 64 | tf_op jit(solution)/shard_map/psum | solution.py:106
  252.9 15.4 %select_reduce_fusion = f32[8,4096]{1,0:T(8,128)S(1)} fusion(s32[8,4096]{1,0:T(8,128)S(1)} %get-tuple-element.23, f32[128,128,1]{1,0,2:T(8,128)S(1)} %bitcast.154, s32[8,4096]{1,0:T(8,128)S(1)} %get-tuple-element.22), kind=kOutput, calls=%fused_computation | convolution fusion | flops 6459195392 | bytes 458752 | tf_op jit(solution)/shard_map/csr,rw->csw/dot_general | solution.py:97
  269.9 123.0 %all-reduce.4.cloned.1.call-done = f32[8,4096]{1,0:T(8,128)} async-done(((f32[8,4096]{1,0:T(8,128)}), f32[8,4096]{1,0:T(8,128)}) %all-reduce.4.cloned.1.call-update) | async-done | bytes 131088 | tf_op jit(solution)/shard_map/psum | solution.py:107
  392.8 1.1 reduce_sum.55
  394.4 1.6 copy.70
  (66 shorter events, 17.2 us)
Async XLA Ops:
  7.2 111.4 %all-reduce.6.cloned.1.call-start = ((), (), s32[]{:S(2)}) async-start(), calls=%async_computation.5 | async-start | bytes 1048576 | tf_op jit(solution)/shard_map/psum | solution.py:9
  41.5 81.6 %all-to-all-start = ((bf16[8,2,4,32,2,128]{5,4,3,2,1,0:T(2,128)(2,1)}), bf16[8,2,4,32,2,128]{5,4,3,2,1,0:T(2,128)(2,1)S(1)}, u32[]{:S(2)}, u32[]{:S(2)}) async-start(bf16[8,2,4,32,2,128]{5,4,3,2,1,0:T(2,128)(2,1)} %param.4), calls=%async_computation | async-start | bytes 2097152 | tf_op jit(solution)/shard_map/all_to_all | solution.py:42
  45.8 165.8 %reduce-scatter.2.cloned.1.call-start = ((), (), s32[]{:S(2)}) async-start(), calls=%async_computation.3 | async-start | bytes 589824 | tf_op jit(solution)/shard_map/reduce_scatter | solution.py:71
  118.6 4.4 %copy-start.3 = (bf16[1,2,128,128]{3,2,0,1:T(8,128)(2,1)S(1)}, bf16[1,2,128,128]{3,2,0,1:T(8,128)(2,1)}, u32[]{:S(2)}) copy-start(bf16[1,2,128,128]{3,2,0,1:T(8,128)(2,1)} %get-tuple-element.18) | copy-start | bytes 196612
  118.6 4.4 %copy-start.2 = (bf16[1,2,128,128]{3,2,0,1:T(8,128)(2,1)S(1)}, bf16[1,2,128,128]{3,2,0,1:T(8,128)(2,1)}, u32[]{:S(2)}) copy-start(bf16[1,2,128,128]{3,2,0,1:T(8,128)(2,1)} %get-tuple-element.19) | copy-start | bytes 196612
  148.9 63.7 %copy-start.1 = (s32[8,4096]{1,0:T(8,128)S(1)}, s32[8,4096]{1,0:T(8,128)}, u32[]{:S(2)}) copy-start(s32[8,4096]{1,0:T(8,128)} %param.7) | copy-start | bytes 393220
  149.8 243.0 %all-reduce.4.cloned.1.call-start = ((), (), s32[]{:S(2)}) async-start(), calls=%async_computation.4 | async-start | bytes 262144 | tf_op jit(solution)/shard_map/psum | solution.py:107
  252.9 16.2 %copy-start = (bf16[4,32,2,128]{3,1,2,0:T(8,128)(2,1)S(1)}, bf16[4,32,2,128]{3,1,2,0:T(8,128)(2,1)}, u32[]{:S(2)}) copy-start(bf16[4,32,2,128]{3,1,2,0:T(8,128)(2,1)} %reduce-scatter.2.cloned.1.call-done) | copy-start | bytes 196612
Sparse Core Ops, SparseCore 0:
  41.6 76.9 all-reduce.5
  149.9 61.5 reduce-scatter.1
  269.3 123.5 all-reduce.3
where the time goes:
time: 403 us; the launch traced here: 402 us
  waiting for transfers between devices  257 us (64%)
  blocking collectives  51.4 us (13%)
  between operations  37.4 us (9%)
  local copies, waits for them, and re-layouts  22.5 us (6%)
  matrix products  19.5 us (5%)
  other arithmetic  9.91 us (2%)
  starting transfers between devices  4.36 us (1%)
    psum x1, waiting for transfers between devices, on_device(): lax.psum(sample_mass * dimension_scale / norm_total[:, None], ('cuts', 'm...  123 us
    psum x1, waiting for transfers between devices, from_root(): return lax.psum(jnp.where(mine, array, jnp.zeros_like(array)), axis)  72.8 us
    reduce_scatter x1, waiting for transfers between devices, on_device(): lax.psum_scatter(summed.astype(jnp.bfloat16), 'cuts', scatter_dimension=0...  61.7 us
    psum x1, blocking collectives, on_device(): norm_total = lax.psum(norm_part, ('cuts', 'mode'))  40.1 us
    dot_general x1, matrix products, on_device(): jnp.einsum('csr,rw->csw', cell_onehot, magnitude.reshape(cell_count, widt...  15.4 us
    all_to_all x1, blocking collectives, on_device(): lax.all_to_all(summed.astype(jnp.bfloat16), 'mode', split_axis=2, concat_...  11.4 us
  transfers between devices with their start and end apart: 4, of which 3 were waited for; matrix products, arithmetic and copies ran while one was open for 1% of the time, Pallas kernels for 0%

commit v1 on v0

v1 whole, which is shorter than its diff:
```python
import functools

import jax
import jax.numpy as jnp
from jax import lax
from jax.experimental import pallas as pl
from jax.experimental.pallas import tpu as pltpu
from jax.sharding import PartitionSpec as P

MESH = pl.DeviceIdType.MESH
BF16 = jnp.bfloat16
F32 = jnp.float32


def dot(a, b):
    return jnp.dot(a, b, preferred_element_type=F32)


def stacked(real_part, imag_part):
    top = jnp.concatenate([real_part, imag_part], axis=1)
    bottom = jnp.concatenate([-imag_part, real_part], axis=1)
    return jnp.concatenate([top, bottom], axis=0)


def kernel(
    cfg,
    x_ref,
    gates_ref,
    samples_ref,
    slot_ref,
    amp_ref,
    probs_ref,
    xeb_ref,
    part,
    got,
    mine,
    whole,
    relay,
    pick,
    blocks,
    plane,
    own,
    land,
    gate_send,
    gate_recv,
    pick_send,
    pick_recv,
    part_send,
    part_recv,
    mode_send,
    mode_recv,
    prob_send,
    prob_recv,
):
    ncuts, nmode, circuits, spect, width, per_circuit = cfg
    ndev = ncuts * nmode
    k = lax.axis_index("cuts")
    m = lax.axis_index("mode")
    me = k * nmode + m
    sharers = ncuts // circuits
    c = k // sharers
    held = gates_ref.shape[0]
    npieces, _, piece = blocks.shape[0], blocks.shape[1], blocks.shape[2]
    rows_out = amp_ref.shape[0]
    pb2 = amp_ref.shape[1]
    ns = own.shape[1]

    barrier = pltpu.get_barrier_semaphore()

    @pl.loop(1, ndev)
    def _(i):
        d = lax.rem(me + i, ndev)
        pl.semaphore_signal(
            barrier, inc=1, device_id=(d // nmode, lax.rem(d, nmode)), device_id_type=MESH
        )

    for i in range(circuits):
        total = x_ref[i, 0].astype(F32)
        for j in range(1, x_ref.shape[1]):
            total = total + x_ref[i, j].astype(F32)
        part[i] = total.astype(BF16)

    pl.semaphore_wait(barrier, ndev - 1)

    def gate_copy(src, dst):
        rows = pl.ds(pl.multiple_of(dst * piece, piece), piece)
        return pltpu.make_async_remote_copy(
            src_ref=gates_ref.at[:, rows],
            dst_ref=relay.at[pl.ds(src * held, held)],
            send_sem=gate_send.at[dst],
            recv_sem=gate_recv.at[src],
            device_id=(dst, m),
            device_id_type=MESH,
        )

    def pick_copy(src, dst):
        return pltpu.make_async_remote_copy(
            src_ref=pick.at[dst // sharers],
            dst_ref=blocks.at[src],
            send_sem=pick_send.at[dst],
            recv_sem=pick_recv.at[src],
            device_id=(dst, m),
            device_id_type=MESH,
        )

    def part_copy(src, dst):
        return pltpu.make_async_remote_copy(
            src_ref=part.at[dst // sharers],
            dst_ref=got.at[src],
            send_sem=part_send.at[dst],
            recv_sem=part_recv.at[src],
            device_id=(dst, m),
            device_id_type=MESH,
        )

    def mode_copy(src, dst):
        return pltpu.make_async_remote_copy(
            src_ref=mine,
            dst_ref=whole.at[src],
            send_sem=mode_send.at[dst],
            recv_sem=mode_recv.at[src],
            device_id=(k, dst),
            device_id_type=MESH,
        )

    def prob_copy(src, dst):
        return pltpu.make_async_remote_copy(
            src_ref=own,
            dst_ref=land.at[src],
            send_sem=prob_send.at[dst],
            recv_sem=prob_recv.at[src],
            device_id=(dst // nmode, lax.rem(dst, nmode)),
            device_id_type=MESH,
        )

    def relays(action):
        if npieces == ncuts:
            action()
        else:
            pl.when(k < npieces)(action)

    for i in range(1, ncuts):
        j = lax.rem(k + i, ncuts)

        def start_gate():
            gate_copy(k, j).start()

        if npieces == ncuts:
            start_gate()
        else:
            pl.when(j < npieces)(start_gate)
    for i in range(1, ncuts):
        part_copy(k, lax.rem(k + i, ncuts)).start()

    def relay_gates():
        rows = pl.ds(pl.multiple_of(k * piece, piece), piece)
        relay[pl.ds(k * held, held)] = gates_ref[:, rows]
        for i in range(1, ncuts):
            gate_copy(lax.rem(k + ncuts - i, ncuts), k).wait_recv()
        for i in range(circuits):
            for b in range(per_circuit):
                pick[i, b] = relay[slot_ref[i * per_circuit + b]]
        for i in range(1, ncuts):
            pick_copy(k, lax.rem(k + i, ncuts)).start()
        blocks[k] = pick[c]

    relays(relay_gates)

    total = part[c].astype(F32)
    for i in range(1, ncuts):
        j = lax.rem(k + ncuts - i, ncuts)
        part_copy(j, k).wait_recv()
        total = total + got[j].astype(F32)
    mine[...] = total.astype(BF16)
    for i in range(1, nmode):
        mode_copy(m, lax.rem(m + i, nmode)).start()
    whole[m] = total.astype(BF16)

    for i in range(1, ncuts):
        j = lax.rem(k + ncuts - i, ncuts)

        def wait_pick():
            pick_copy(j, k).wait_recv()

        if npieces == ncuts:
            wait_pick()
        else:
            pl.when(j < npieces)(wait_pick)

    def block(b):
        return blocks[:, b].reshape(2 * width, width)

    def composed(kind):
        left = None
        for b in range(kind, per_circuit, 2):
            gate = block(b)
            real_part, imag_part = gate[:width], gate[width:]
            if left is None:
                left = jnp.concatenate([real_part, imag_part], axis=1)
            else:
                left = dot(left, stacked(real_part, imag_part)).astype(BF16)
        return left[:, :width], left[:, width:]

    right = stacked(*composed(0))
    col_real, col_imag = composed(1)
    left_t = stacked(col_real, col_imag).astype(F32).T.astype(BF16)

    for i in range(1, nmode):
        mode_copy(lax.rem(m + nmode - i, nmode), m).wait_recv()

    for s in range(spect):
        for j in range(nmode):
            plane[s, j * pb2 : (j + 1) * pb2] = whole[j, s * pb2 : (s + 1) * pb2].astype(F32)
    state = jnp.concatenate(
        [
            jnp.concatenate(
                [plane[s, pl.ds(0, width, stride=2), :], plane[s, pl.ds(1, width, stride=2), :]],
                axis=1,
            )
            for s in range(spect)
        ],
        axis=0,
    ).astype(BF16)
    state = dot(state, right).astype(BF16)
    state = jnp.concatenate(
        [
            jnp.concatenate(
                [
                    state[s * width : (s + 1) * width, r * width : (r + 1) * width]
                    for s in range(spect)
                ],
                axis=1,
            )
            for r in range(2)
        ],
        axis=0,
    )
    out = dot(left_t, state)
    magnitude = out[:width] * out[:width] + out[width:] * out[width:]
    norm = jnp.sum(jnp.sum(magnitude, axis=0, keepdims=True), axis=1, keepdims=True)

    table = jnp.concatenate(
        [magnitude[:, s * width : (s + 1) * width] for s in range(spect)], axis=0
    )
    high = table.astype(BF16)
    low = (table - high.astype(F32)).astype(BF16)
    table_t = jnp.concatenate([high, low], axis=1)
    group = lax.rem(k, sharers) * nmode + m
    chunk = samples_ref[:, pl.ds(pl.multiple_of(group * ns, ns), ns)]
    ours = lax.broadcasted_iota(jnp.int32, chunk.shape, 0) == c
    wanted = jnp.sum(jnp.where(ours, chunk, 0), axis=0, keepdims=True)
    row_id = wanted // width
    col_id = wanted - row_id * width
    row_hot = (
        (lax.broadcasted_iota(jnp.int32, (spect * width, ns), 0) == row_id)
        .astype(F32)
        .astype(BF16)
    )
    found = lax.dot_general(
        table_t, row_hot, (((0,), (0,)), ((), ())), preferred_element_type=F32
    )
    found = found[:width] + found[width:]
    col_hot = lax.broadcasted_iota(jnp.int32, (width, ns), 0) == col_id
    mass = jnp.sum(jnp.where(col_hot, found, 0.0), axis=0, keepdims=True)
    prob = mass * float(spect * width * width) / norm
    own[...] = prob
    land[me] = prob

    @pl.loop(1, ndev)
    def _(i):
        prob_copy(me, lax.rem(me + i, ndev)).start()

    for s in range(spect):
        for r in range(2):
            plane[s, pl.ds(r, width, stride=2), :] = out[
                r * width : (r + 1) * width, s * width : (s + 1) * width
            ]
    first = lax.rem(k, sharers) * rows_out
    amp_ref[...] = plane[pl.ds(first, rows_out), pl.ds(pl.multiple_of(m * pb2, pb2), pb2), :]

    for i in range(1, ncuts):
        j = lax.rem(k + i, ncuts)

        def end_gate():
            gate_copy(k, j).wait_send()

        if npieces == ncuts:
            end_gate()
        else:
            pl.when(j < npieces)(end_gate)

        def end_pick():
            pick_copy(k, j).wait_send()

        relays(end_pick)
        part_copy(k, j).wait_send()
    for i in range(1, nmode):
        mode_copy(m, lax.rem(m + i, nmode)).wait_send()

    @pl.loop(1, ndev)
    def _(i):
        prob_copy(me, lax.rem(me + i, ndev)).wait_send()
        prob_copy(lax.rem(me + ndev - i, ndev), me).wait_recv()

    for d in range(ndev):
        dk, dm = d // nmode, d % nmode
        dc = dk // sharers
        at = (dk % sharers * nmode + dm) * ns
        probs_ref[dc : dc + 1, at : at + ns] = land[d]
    xeb_ref[...] = jnp.broadcast_to(
        jnp.mean(probs_ref[...], axis=1, keepdims=True), xeb_ref.shape
    )


def on_device(mesh, sliced_state, gate_blocks, gate_slot, samples):
    ncuts, nmode = mesh.shape["cuts"], mesh.shape["mode"]
    ndev = ncuts * nmode
    circuits, local_slices, spect, pb, _, width = sliced_state.shape
    held = gate_blocks.shape[0]
    nblk = gate_slot.shape[0]
    per_circuit = nblk // circuits
    assert ncuts % circuits == 0
    sharers = ncuts // circuits
    assert spect % sharers == 0
    rows_out = spect // sharers
    nsamples = samples.shape[1]
    ns = nsamples // (sharers * nmode)
    npieces = min(ncuts, 2 * width // 16)
    piece = 2 * width // npieces
    rows = spect * pb * 2
    cfg = (ncuts, nmode, circuits, spect, width, per_circuit)
    vmem = pl.BlockSpec(memory_space=pltpu.VMEM)
    dma = pltpu.SemaphoreType.DMA
    amplitudes, probs, xeb = pl.pallas_call(
        functools.partial(kernel, cfg),
        out_shape=[
            jax.ShapeDtypeStruct((rows_out, pb * 2, width), F32),
            jax.ShapeDtypeStruct((circuits, nsamples), F32),
            jax.ShapeDtypeStruct((circuits, 128), F32),
        ],
        in_specs=[vmem, vmem, vmem, pl.BlockSpec(memory_space=pltpu.SMEM)],
        out_specs=[vmem, vmem, vmem],
        scratch_shapes=[
            pltpu.VMEM((circuits, rows, width), BF16),
            pltpu.VMEM((ncuts, rows, width), BF16),
            pltpu.VMEM((rows, width), BF16),
            pltpu.VMEM((nmode, rows, width), BF16),
            pltpu.VMEM((nblk, piece, width), BF16),
            pltpu.VMEM((circuits, per_circuit, piece, width), BF16),
            pltpu.VMEM((npieces, per_circuit, piece, width), BF16),
            pltpu.VMEM((spect, 2 * width, width), F32),
            pltpu.VMEM((1, ns), F32),
            pltpu.VMEM((ndev, 1, ns), F32),
            dma((ncuts,)),
            dma((ncuts,)),
            dma((ncuts,)),
            dma((ncuts,)),
            dma((ncuts,)),
            dma((ncuts,)),
            dma((nmode,)),
            dma((nmode,)),
            dma((ndev,)),
            dma((ndev,)),
        ],
        compiler_params=pltpu.CompilerParams(collective_id=0, has_side_effects=True),
    )(
        sliced_state.reshape(circuits, local_slices, rows, width),
        gate_blocks.reshape(held, 2 * width, width),
        samples,
        gate_slot,
    )
    return (amplitudes.reshape(rows_out, pb, 2, width), probs, xeb[:, 0])


def solution(mesh):
    in_specs = (P(None, "cuts", None, "mode", None, None), P("cuts", None, None, None), P(), P())
    out_specs = (P("cuts", "mode", None, None), P(), P())
    return jax.shard_map(
        functools.partial(on_device, mesh),
        mesh=mesh,
        in_specs=in_specs,
        out_specs=out_specs,
        check_vma=False,
    )
```

time: 403 us -> 46.8 us (0.12)
  waiting for transfers between devices: 257 us -> 0 us
  blocking collectives: 51.4 us -> 0 us
  Pallas kernels: 0 us -> 42.4 us
  between operations: 37.4 us -> 0.65 us
  matrix products: 19.5 us -> 0 us
  local copies, waits for them, and re-layouts: 22.5 us -> 3.56 us
  other arithmetic: 9.91 us -> 0 us
  starting transfers between devices: 4.36 us -> 0 us
    psum x2 -> x0, waiting for transfers between devices: 196 us -> none  [the longest x1 123 us: on_device(): lax.psum(sample_mass * dimension_scale / norm_total[:, None], ('cuts', 'm...]
    reduce_scatter x1 -> x0, waiting for transfers between devices: 61.7 us -> none  [on_device(): lax.psum_scatter(summed.astype(jnp.bfloat16), 'cuts', scatter_dimension=0...]
    pallas_call x0 -> x1, Pallas kernels: none -> 42.4 us  [on_device(): pl.pallas_call(functools.partial(kernel, cfg), out_shape=[jax.ShapeDtypeS...]
    psum x1 -> x0, blocking collectives: 40.1 us -> none  [on_device(): norm_total = lax.psum(norm_part, ('cuts', 'mode'))]
    dot_general x13 -> x0, matrix products: 19.5 us -> none  [the longest x1 15.4 us: on_device(): jnp.einsum('csr,rw->csw', cell_onehot, magnitude.reshape(cell_count, widt...]
    all_to_all x1 -> x0, blocking collectives: 11.4 us -> none  [on_device(): lax.all_to_all(summed.astype(jnp.bfloat16), 'mode', split_axis=2, concat_...]
    reshape x8 -> x0, local copies, waits for them, and re-layouts: 4.47 us -> none  [the longest x4 2.84 us: apply_gates(): flattened = tensor.reshape(layout[0], -1, 2 * layout[-1])]
    all_to_all x1 -> x0, starting transfers between devices: 4.28 us -> none  [on_device(): lax.all_to_all(sliced_state, 'mode', split_axis=0, concat_axis=3, tiled=T...]
  transfers between devices with their start and end apart: 4 -> 0, of which waited for: 3 -> 0; matrix products, arithmetic and copies ran while one was open for 1% -> 0% of each run, Pallas kernels for 0% -> 0%
where the time goes in v1:
time: 46.8 us; the launch traced here: 46.6 us
  Pallas kernels  42.4 us (91%)
  local copies, waits for them, and re-layouts  3.56 us (8%)
  between operations  0.65 us (1%)
    pallas_call x1, Pallas kernels, on_device(): pl.pallas_call(functools.partial(kernel, cfg), out_shape=[jax.ShapeDtypeS...  42.4 us
    unnamed x6, local copies, waits for them, and re-layouts  2.94 us

profile of v1, /device:TPU:0, one launch (start us, length us, event | category | flops | bytes accessed | tf_op | source)
XLA Modules:
  0.0 46.6 jit_solution(17449758143173558782)
XLA Ops:
  0.6 42.4 %shard_map.67 = (f32[4,64,128]{2,1,0:T(8,128)}, f32[8,4096]{1,0:T(8,128)}, f32[8,128]{1,0:T(8,128)}) custom-call(bf16[8,2,256,128]{3,2,1,0:T(8,128)(2,1)} %bitcast.3, bf16[4,256,128]{2,1,0:T(8,128)(2,1)} %bitcast.4, s32[8,4096]{1,0:T(8,128)} %samples_ref.1, s32[32]{0:T(128)} %slot_ref.1), custom_call_target="tpu_custom_call" | custom-call | tf_op jit(solution)/shard_map/pallas_call | solution.py:334
  43.1 0.0 copy-start.1
  43.1 0.7 %copy-done.1 = f32[8,128]{1,0:T(8,128)S(1)} copy-done((f32[8,128]{1,0:T(8,128)S(1)}, f32[8,128]{1,0:T(8,128)}, u32[]{:S(2)}) %copy-start.1) | copy-done | bytes 4120
  43.8 0.6 %slice_reduce_fusion = f32[8]{0:T(128)} fusion(f32[8,128]{1,0:T(8,128)S(1)} %copy-done.1), kind=kLoop, calls=%fused_computation | loop fusion | bytes 64 | tf_op jit(solution)/shard_map/slice | solution.py:372
  44.4 0.0 copy-start
  44.4 1.6 %copy.9 = f32[4,32,2,128]{3,2,1,0:T(2,128)} copy(f32[4,32,2,128]{3,2,1,0:T(2,128)} %bitcast.5) | data formatting | bytes 262144
  46.0 0.0 copy-done
  46.0 0.7 %copy.10 = f32[8,4096]{1,0:T(8,128)} copy(f32[8,4096]{1,0:T(8,128)S(1)} %copy-done) | data formatting | bytes 262144
Async XLA Ops:
  43.1 0.7 %copy-start.1 = (f32[8,128]{1,0:T(8,128)S(1)}, f32[8,128]{1,0:T(8,128)}, u32[]{:S(2)}) copy-start(f32[8,128]{1,0:T(8,128)} %get-tuple-element.8) | copy-start | bytes 12292
  44.4 1.6 %copy-start = (f32[8,4096]{1,0:T(8,128)S(1)}, f32[8,4096]{1,0:T(8,128)}, u32[]{:S(2)}) copy-start(f32[8,4096]{1,0:T(8,128)} %get-tuple-element.13) | copy-start | bytes 393220
